TPU v7x, 32 devices: a whole 2x2x4 slice. The times are simulated.
32 devices in a mesh: fsdp: 4 (over z), ctx: 2 (over x), tp: 4 (over y, core).
Axes of the slice: x: 2, y: 2, z: 4, core: 2. Of those that a mesh axis runs over, the one named last changes fastest.
Arguments:
- residual: bfloat16 [8, 1024, 1024], P('fsdp', ('ctx', 'tp')), may hold values from -6 to 6
- query_weight: bfloat16 [1024, 1024], P('fsdp', 'tp'), may hold values from -0.1875 to 0.1875
- key_weight: bfloat16 [1024, 1024], P('fsdp', 'tp'), may hold values from -0.1875 to 0.1875
- value_weight: bfloat16 [1024, 1024], P('fsdp', 'tp'), may hold values from -0.1875 to 0.1875
- output_weight: bfloat16 [1024, 1024], P('tp', 'fsdp'), may hold values from -0.1875 to 0.1875
- sharpness: float32 [1024], P('tp'), may hold values from 1 to 1.8
- attend_rate: float32 [1024], replicated, may hold values from 0.15 to 0.9
- up_weight: bfloat16 [1024, 4096], P('fsdp', 'tp'), may hold values from -0.1875 to 0.1875
- gate_weight: bfloat16 [1024, 4096], P('fsdp', 'tp'), may hold values from -0.1875 to 0.1875
- down_weight: bfloat16 [4096, 1024], P('tp', 'fsdp'), may hold values from -0.09375 to 0.09375
- amplitude: float32 [4096], P('tp'), may hold values from 0.5 to 2
- steepness: float32 [4096], P('tp'), may hold values from 0.5 to 2
- mixer_rate: float32 [1024], replicated, may hold values from 0.15 to 0.9
- block_ids: int32 [8, 1024], P('fsdp'), may hold values from 0 to 4, as said below
- positions: int32 [8, 1024], P('fsdp', 'ctx'), may hold values from 0 to 4095
- cotangent: bfloat16 [8, 1024, 1024], P('fsdp', ('ctx', 'tp')), may hold values from -6 to 6
Outputs:
- layer_out: bfloat16 [8, 1024, 1024], P('fsdp', ('ctx', 'tp'))
- grad_input: float32 [8, 1024, 1024], P('fsdp', ('ctx', 'tp'))
- grad_query: float32 [1024, 1024], P('fsdp', 'tp')
- grad_key: float32 [1024, 1024], P('fsdp', 'tp')
- grad_value: float32 [1024, 1024], P('fsdp', 'tp')
- grad_output: float32 [1024, 1024], P('tp', 'fsdp')
- grad_sharpness: float32 [1024], replicated
- grad_attend: float32 [1024], replicated
- grad_up: float32 [1024, 4096], P('fsdp', 'tp')
- grad_gate: float32 [1024, 4096], P('fsdp', 'tp')
- grad_down: float32 [4096, 1024], P('tp', 'fsdp')
- grad_amplitude: float32 [4096], replicated
- grad_steepness: float32 [4096], replicated
- grad_mixer: float32 [1024], replicated
Inputs may be any that keep to these rules, and one draw needn't show every extreme that they name: `block_ids`: in each sequence the block id of the token at index t is (t + offset) // 256, with an offset of 1 to 255 drawn for each sequence: full blocks of 256 tokens, a shorter first and last block.
All inputs are finite; a program needn't handle non-finite values.
Results may differ from a plain program's by a relative error of at most 0.02.
Values may be sent and summed in bfloat16 or wider, within the bound.
A program may use at most 128 MiB of HBM per device.

v0:
```python
import math
import jax
import jax.numpy as jnp
from jax import lax
from jax.sharding import PartitionSpec as P

HD = 64
norm_eps = 1e-06
rope_base = 10000.0
BF = jnp.bfloat16
F32 = jnp.float32


def unit_rows(values):
    return values * lax.rsqrt(jnp.mean(values * values, axis=-1, keepdims=True) + norm_eps)


def rotate_pairs(values, angles):
    middle = values.shape[-1] // 2
    leading = values[..., :middle]
    trailing = values[..., middle:]
    cosine = jnp.cos(angles)[..., None, :]
    sine_part = jnp.sin(angles)[..., None, :]
    return jnp.concatenate(
        [leading * cosine - trailing * sine_part, trailing * cosine + leading * sine_part], axis=-1
    )


def angles_for(positions, head_size):
    middle = head_size // 2
    frequency = rope_base ** (-2.0 * jnp.arange(middle).astype(F32) / head_size)
    return positions.astype(F32)[..., None] * frequency


def prepare_heads(projected, angles, gains, head_size):
    heads_here = projected.shape[-1] // head_size
    shaped = projected.reshape(projected.shape[:-1] + (heads_here, head_size))
    normed = unit_rows(rotate_pairs(shaped, angles)) * gains.reshape(heads_here, head_size)
    return normed.reshape(projected.shape)


def product(left, right):
    return jnp.dot(left, right, preferred_element_type=F32)


def transposed_left(left, right):
    return lax.dot_general(left, right, (((0,), (0,)), ((), ())), preferred_element_type=F32)


def transposed_right(left, right):
    return lax.dot_general(left, right, (((1,), (1,)), ((), ())), preferred_element_type=F32)


def gather_rows(values):
    return lax.all_gather(values, "tp", axis=1, tiled=True)


def reduce_rows(values):
    return lax.psum_scatter(values.astype(BF), "tp", scatter_dimension=1, tiled=True).astype(F32)


def branch_mix(branch, base, rate):
    return unit_rows(base + rate * (unit_rows(branch) - base))


def activate(upper, gated_raw, amplitude, steepness):
    scaled = gated_raw * steepness
    return upper * amplitude * (scaled * jax.nn.sigmoid(scaled))


def trade(values, sizes):
    n = sizes["ctx"]
    me = lax.axis_index("ctx")
    if n == 2:
        own = lax.dynamic_index_in_dim(values, me, 0, keepdims=False)
        other = lax.dynamic_index_in_dim(values, 1 - me, 0, keepdims=False)
        got = lax.ppermute(other, "ctx", [(0, 1), (1, 0)])
        first = jnp.where(me == 0, own, got)
        second = jnp.where(me == 0, got, own)
        return jnp.stack([first, second])
    return lax.all_to_all(values, "ctx", split_axis=0, concat_axis=0, tiled=True)


def attend_both(query_low, key_low, value_low, ids):
    length, width = query_low.shape
    heads = width // HD
    q = query_low.reshape(length, heads, HD)
    k = key_low.reshape(length, heads, HD)
    v = value_low.reshape(length, heads, HD)
    scores = jnp.einsum("qhd,khd->hqk", q, k, preferred_element_type=F32) / math.sqrt(HD)
    allowed = ids[None, :] <= ids[:, None]
    scores = jnp.where(allowed[None], scores, -1e30)
    row_max = jnp.max(scores, axis=-1, keepdims=True)
    exponent = jnp.exp(scores - row_max)
    row_total = jnp.sum(exponent, axis=-1, keepdims=True)
    weights_low = (exponent / row_total).astype(BF)
    out = jnp.einsum("hqk,khd->qhd", weights_low, v, preferred_element_type=F32)
    return (out.reshape(length, width).astype(BF), (row_max + jnp.log(row_total))[..., 0])


def attend_back(query_low, key_low, value_low, ids, logsum, grad):
    length, width = query_low.shape
    heads = width // HD
    q = query_low.reshape(length, heads, HD)
    k = key_low.reshape(length, heads, HD)
    v = value_low.reshape(length, heads, HD)
    g = grad.reshape(length, heads, HD)
    scores = jnp.einsum("qhd,khd->hqk", q, k, preferred_element_type=F32) / math.sqrt(HD)
    allowed = ids[None, :] <= ids[:, None]
    scores = jnp.where(allowed[None], scores, -1e30)
    soft = jnp.exp(scores - logsum[..., None])
    grad_v = jnp.einsum("hqk,qhd->khd", soft.astype(BF), g, preferred_element_type=F32)
    grad_w = jnp.einsum("qhd,khd->hqk", g, v, preferred_element_type=F32)
    grad_s = soft * (grad_w - jnp.sum(grad_w * soft, axis=-1, keepdims=True))
    low = grad_s.astype(BF)
    grad_q = jnp.einsum("hqk,khd->qhd", low, k, preferred_element_type=F32) / math.sqrt(HD)
    grad_k = jnp.einsum("hqk,qhd->khd", low, q, preferred_element_type=F32) / math.sqrt(HD)
    return (
        grad_q.reshape(length, width),
        grad_k.reshape(length, width),
        grad_v.reshape(length, width),
    )


def per_device(sizes):

    def run(
        residual,
        query_weight,
        key_weight,
        value_weight,
        output_weight,
        sharpness,
        attend_rate,
        up_weight,
        gate_weight,
        down_weight,
        amplitude,
        steepness,
        mixer_rate,
        block_ids,
        positions,
        cotangent,
    ):
        z = sizes["fsdp"]
        width = residual.shape[2]
        hidden_here = up_weight.shape[1]
        heads_width = query_weight.shape[1]
        mine = trade(residual, sizes)
        qkv_shard = jnp.concatenate([query_weight, key_weight, value_weight], axis=1)
        full_qkv = lax.all_gather(qkv_shard, "fsdp", axis=0, tiled=True)
        full_output = lax.all_gather(output_weight, "fsdp", axis=1, tiled=True)
        ug_shard = jnp.concatenate([up_weight, gate_weight], axis=1)
        full_ug = lax.all_gather(ug_shard, "fsdp", axis=0, tiled=True)
        full_down = lax.all_gather(down_weight, "fsdp", axis=1, tiled=True)
        ctx = lax.axis_index("ctx")
        ids = lax.dynamic_index_in_dim(block_ids, ctx, 0, keepdims=False)
        all_positions = lax.all_gather(positions, "ctx", axis=1, tiled=True)
        my_positions = lax.dynamic_index_in_dim(all_positions, ctx, 0, keepdims=False)
        angles = angles_for(my_positions, HD)
        gathered = gather_rows(mine)
        shape3 = gathered.shape
        flat_in = gathered.reshape(-1, width)
        raw = product(flat_in, full_qkv)
        raw_query, raw_key, raw_value = jnp.split(raw, 3, axis=1)

        def prepare_local(projected, gains):
            return prepare_heads(projected, angles, gains, HD)

        query_ready, query_back = jax.vjp(prepare_local, raw_query, sharpness)
        key_ready, key_back = jax.vjp(prepare_local, raw_key, sharpness)
        query_low = query_ready.astype(BF)
        key_low = key_ready.astype(BF)
        value_low = raw_value.astype(BF)
        attended, logsum = attend_both(query_low, key_low, value_low, ids)
        attend_sum = reduce_rows(product(attended, full_output).reshape(shape3))
        residual_float = mine.astype(F32)
        first, attend_back_mix = jax.vjp(branch_mix, attend_sum, residual_float, attend_rate)
        first_all = gather_rows(first.astype(BF)).reshape(-1, width)
        ug_raw = product(first_all, full_ug)
        up_raw, gate_raw = (ug_raw[:, :hidden_here], ug_raw[:, hidden_here:])
        hidden, activate_back = jax.vjp(activate, up_raw, gate_raw, amplitude, steepness)
        hidden_low = hidden.astype(BF)
        down_sum = reduce_rows(product(hidden_low, full_down).reshape(shape3))
        outcome, mixer_back = jax.vjp(branch_mix, down_sum, first, mixer_rate)
        layer_out = trade(outcome.astype(BF), sizes)
        my_cot = trade(cotangent, sizes)
        grad_down_sum, grad_first, grad_mixer_part = mixer_back(my_cot.astype(F32))
        down_grad_all = gather_rows(grad_down_sum.astype(BF)).reshape(-1, width)
        grad_hidden = transposed_right(down_grad_all, full_down)
        grad_down_part = transposed_left(hidden_low, down_grad_all)
        grad_up_raw, grad_gate_raw, grad_amplitude_part, grad_steepness_part = activate_back(
            grad_hidden
        )
        ug_grad = jnp.concatenate([grad_up_raw.astype(BF), grad_gate_raw.astype(BF)], axis=1)
        first_back = transposed_right(ug_grad, full_ug)
        grad_first = grad_first + reduce_rows(first_back.reshape(shape3))
        grad_ug_part = transposed_left(first_all, ug_grad)
        grad_attend_sum, grad_residual, grad_attend_part = attend_back_mix(grad_first)
        attend_grad_all = gather_rows(grad_attend_sum.astype(BF)).reshape(-1, width)
        grad_output_part = transposed_left(attended, attend_grad_all)
        grad_attended = transposed_right(attend_grad_all, full_output).astype(BF)
        grad_query_ready, grad_key_ready, grad_value_ready = attend_back(
            query_low, key_low, value_low, ids, logsum, grad_attended
        )
        grad_raw_query, sharp_query = query_back(grad_query_ready)
        grad_raw_key, sharp_key = key_back(grad_key_ready)
        qkv_grad = jnp.concatenate(
            [grad_raw_query.astype(BF), grad_raw_key.astype(BF), grad_value_ready.astype(BF)],
            axis=1,
        )
        input_back = transposed_right(qkv_grad, full_qkv)
        grad_input = grad_residual + reduce_rows(input_back.reshape(shape3))
        grad_input = trade(grad_input.astype(BF), sizes).astype(F32)
        grad_qkv_part = transposed_left(flat_in, qkv_grad)

        def sum_rows(part):
            share = lax.psum_scatter(
                part.astype(BF), ("fsdp", "ctx"), scatter_dimension=0, tiled=True
            )
            return lax.all_gather(share, "ctx", axis=0, tiled=True).astype(F32)

        def sum_columns(part):
            share = lax.psum_scatter(
                part.astype(BF), ("fsdp", "ctx"), scatter_dimension=1, tiled=True
            )
            return lax.all_gather(share, "ctx", axis=1, tiled=True).astype(F32)

        grad_down = sum_columns(grad_down_part)
        grad_ug = sum_rows(grad_ug_part)
        grad_output = sum_columns(grad_output_part)
        grad_qkv = sum_rows(grad_qkv_part)
        grad_up, grad_gate = (grad_ug[:, :hidden_here], grad_ug[:, hidden_here:])
        grad_query, grad_key, grad_value = jnp.split(grad_qkv, 3, axis=1)
        tensor_index = lax.axis_index("tp")
        tp = sizes["tp"]

        def spread_slice(section):
            return lax.dynamic_update_slice_in_dim(
                jnp.zeros((section.shape[0] * tp,), F32),
                section,
                tensor_index * section.shape[0],
                0,
            )

        grad_sharpness, grad_amplitude, grad_steepness, grad_attend, grad_mixer = lax.psum(
            (
                spread_slice(sharp_query + sharp_key),
                spread_slice(grad_amplitude_part),
                spread_slice(grad_steepness_part),
                grad_attend_part,
                grad_mixer_part,
            ),
            ("fsdp", "ctx", "tp"),
        )
        return (
            layer_out,
            grad_input,
            grad_query,
            grad_key,
            grad_value,
            grad_output,
            grad_sharpness,
            grad_attend,
            grad_up,
            grad_gate,
            grad_down,
            grad_amplitude,
            grad_steepness,
            grad_mixer,
        )

    return run


def solution(mesh):
    return jax.shard_map(
        per_device(dict(mesh.shape)),
        mesh=mesh,
        in_specs=(
            P("fsdp", ("ctx", "tp"), None),
            P("fsdp", "tp"),
            P("fsdp", "tp"),
            P("fsdp", "tp"),
            P("tp", "fsdp"),
            P("tp"),
            P(),
            P("fsdp", "tp"),
            P("fsdp", "tp"),
            P("tp", "fsdp"),
            P("tp"),
            P("tp"),
            P(),
            P("fsdp", None),
            P("fsdp", "ctx"),
            P("fsdp", ("ctx", "tp"), None),
        ),
        out_specs=(
            P("fsdp", ("ctx", "tp"), None),
            P("fsdp", ("ctx", "tp"), None),
            P("fsdp", "tp"),
            P("fsdp", "tp"),
            P("fsdp", "tp"),
            P("tp", "fsdp"),
            P(),
            P(),
            P("fsdp", "tp"),
            P("fsdp", "tp"),
            P("tp", "fsdp"),
            P(),
            P(),
            P(),
        ),
        check_vma=False,
    )
```

profile of v0, /device:TPU:0, one launch (start us, length us, event | category | flops | bytes accessed | tf_op | source)
XLA Modules:
  0.0 814.9 jit_solution(5183301861423763717)
XLA Ops:
  7.3 1.8 pad_maximum_fusion.14
  10.2 3.0 collective-permute-start
  13.2 6.3 collective-permute-done
  21.6 4.3 all_gather.41
  25.9 23.3 %all_gather.42 = bf16[256,1024]{1,0:T(8,128)(2,1)S(1)} all-gather(bf16[256,256]{1,0:T(8,128)(2,1)S(1)} %copy-done.32), channel_id=1, replica_groups=mesh['fsdp'=4,'ctx'=2,'tp'=4] {'fsdp'}, dimensions={1}, use_global_device_ids=true | all-gather | bytes 655360 | tf_op jit(solution)/shard_map/all_gather | solution.py:152
  49.8 1.6 broadcast_compare_fusion
  51.4 7.0 all-gather.11.cloned.1.call-done
  58.4 23.6 %all-gather.9.cloned.1.call-done = bf16[2,512,1024]{2,1,0:T(8,128)(2,1)} async-done(((bf16[2,128,1024]{2,1,0:T(8,128)(2,1)}), bf16[2,512,1024]{2,1,0:T(8,128)(2,1)}) %all-gather.9.cloned.1.call-update) | async-done | bytes 2097168 | tf_op jit(solution)/shard_map/all_gather | solution.py:55
  82.0 3.9 fusion.54
  87.5 7.7 fusion.53
  95.2 8.0 fusion
  103.2 8.2 %fusion.14 = bf16[4,64,1024]{2,1,0:T(8,128)(2,1)} fusion(bf16[1024,4,64]{0,2,1:T(8,128)(2,1)S(1)} %bitcast.135, f32[4,1024,1024]{1,2,0:T(8,128)} %get-tuple-element.74, f32[4,1024]{1,0:T(4,128)S(1)} %fusion, f32[4,1024]{1,0:T(4,128)S(1)} %get-tuple-element.73), kind=kOutput, calls=%fused_computation.55 | convolution fusion | flops 549715968 | bytes 17858560 | tf_op jit(solution)/shard_map/hqk,khd->qhd/dot_general | solution.py:97
  112.8 2.1 convolution_convert_fusion.3
  115.0 2.3 pad_maximum_fusion.8
  117.5 28.8 %reduce-scatter.13.cloned.1.call-done = bf16[2,128,1024]{2,1,0:T(8,128)(2,1)} async-done(((bf16[2,512,1024]{2,1,0:T(8,128)(2,1)}), bf16[2,128,1024]{2,1,0:T(8,128)(2,1)}) %reduce-scatter.13.cloned.1.call-update) | async-done | bytes 524304 | tf_op jit(solution)/shard_map/reduce_scatter | solution.py:59
  149.6 2.2 multiply_convert_fusion.7
  152.5 76.5 %all-gather.15.cloned.1.call-done = bf16[1024,2048]{1,0:T(8,128)(2,1)} async-done(((bf16[256,2048]{1,0:T(8,128)(2,1)}), bf16[1024,2048]{1,0:T(8,128)(2,1)}) %all-gather.15.cloned.1.call-update) | async-done | bytes 4194320 | tf_op jit(solution)/shard_map/all_gather | solution.py:154
  229.0 23.1 %all-gather.13.cloned.1.call-done = bf16[2,512,1024]{2,1,0:T(8,128)(2,1)} async-done(((bf16[2,128,1024]{2,1,0:T(8,128)(2,1)}), bf16[2,512,1024]{2,1,0:T(8,128)(2,1)}) %all-gather.13.cloned.1.call-update) | async-done | bytes 2097168 | tf_op jit(solution)/shard_map/all_gather | solution.py:55
  252.1 6.9 fusion.55
  259.1 3.3 copy-done.9
  262.4 2.3 multiply_convert_fusion.3
  264.7 35.1 %all-gather.17.cloned.1.call-done = bf16[1024,1024]{1,0:T(8,128)(2,1)} async-done(((bf16[1024,256]{1,0:T(8,128)(2,1)}), bf16[1024,1024]{1,0:T(8,128)(2,1)}) %all-gather.17.cloned.1.call-update) | async-done | bytes 2097168 | tf_op jit(solution)/shard_map/all_gather | solution.py:155
  299.8 5.9 convolution_convert_fusion.2
  305.8 1.5 collective-permute-start.2
  307.3 6.4 collective-permute-done.2
  314.7 20.5 %reduce-scatter.15.cloned.1.call-done = bf16[2,128,1024]{2,1,0:T(8,128)(2,1)} async-done(((bf16[2,512,1024]{2,1,0:T(8,128)(2,1)}), bf16[2,128,1024]{2,1,0:T(8,128)(2,1)}) %reduce-scatter.15.cloned.1.call-update) | async-done | bytes 524304 | tf_op jit(solution)/shard_map/reduce_scatter | solution.py:59
  336.6 1.9 fusion.15
  338.5 2.4 fusion.22
  341.0 1.8 fusion.16
  343.0 22.4 %all-gather.19.cloned.1.call-done = bf16[2,512,1024]{2,1,0:T(8,128)(2,1)} async-done(((bf16[2,128,1024]{2,1,0:T(8,128)(2,1)}), bf16[2,512,1024]{2,1,0:T(8,128)(2,1)}) %all-gather.19.cloned.1.call-update) | async-done | bytes 2097168 | tf_op jit(solution)/shard_map/all_gather | solution.py:55
  365.5 9.4 %multiply_reduce_fusion.1 = (f32[1024]{0:T(1024)}, f32[1024]{0:T(1024)}, f32[1024,1024]{1,0:T(8,128)S(1)}, bf16[1024,1024]{1,0:T(8,128)(2,1)S(1)}) fusion(f32[1024,2048]{1,0:T(8,128)} %copy-done.9, f32[1024]{0:T(1024)} %param.27, f32[1024]{0:T(1024)} %param.26, bf16[1024,1024]{1,0:T(8,128)(2,1)} %bitcast.157, ...), kind=kOutput, calls=%fused_computation.15 | convolution fusion | flops 2168453120 | bytes 18890752 | tf_op jit(solution)/shard_map/dot_general | solution.py:51
  375.5 3.1 copy-done.56
  378.6 5.8 fusion.10
  384.4 31.3 %reduce-scatter.17.cloned.1.call-done = bf16[2,128,1024]{2,1,0:T(8,128)(2,1)} async-done(((bf16[2,512,1024]{2,1,0:T(8,128)(2,1)}), bf16[2,128,1024]{2,1,0:T(8,128)(2,1)}) %reduce-scatter.17.cloned.1.call-update) | async-done | bytes 524304 | tf_op jit(solution)/shard_map/reduce_scatter | solution.py:59
  415.7 2.8 multiply_reduce_fusion.3
  419.2 2.7 multiply_reduce_fusion.4
  424.0 9.4 %convolution_convert_fusion = bf16[1024,2048]{1,0:T(8,128)(2,1)} fusion(bf16[1024,1024]{1,0:T(8,128)(2,1)} %bitcast.156, bf16[1024,1024]{1,0:T(8,128)(2,1)} %copy-done.18, bf16[1024,1024]{1,0:T(8,128)(2,1)} %copy-done.59), kind=kOutput, calls=%fused_computation.24 | convolution fusion | flops 4305453056 | bytes 10485760 | tf_op jit(solution)/shard_map/dot_general | solution.py:47
  434.2 5.9 convolution_convert_fusion.1
  440.1 4.0 copy.46
  444.2 2.5 all-gather.21.cloned.1.call-done
  446.7 2.5 convolution_convert_fusion.7
  449.2 1.9 convolution_convert_fusion.6
  452.2 13.7 %multiply_reduce_fusion = (f32[4,1024]{1,0:T(4,128)S(1)}, f32[4,1024,1024]{1,2,0:T(8,128)}) fusion(f32[4,1024,1024]{1,2,0:T(8,128)} %get-tuple-element.74, f32[4,1024]{1,0:T(4,128)S(1)} %log_add_fusion, bf16[1024,4,64]{0,2,1:T(8,128)(2,1)S(1)} %bitcast.133, bf16[1024,4,64]{0,2,1:T(8,128)(2,1)} %bitcast.136), kind=kOutput, calls=%fused_computation.1 | convolution fusion | flops 549449728 | bytes 34635776 | tf_op jit(solution)/shard_map/qhd,khd->hqk/dot_general | solution.py:113
  469.5 10.9 %multiply_convert_fusion = bf16[4,1024,1024]{1,2,0:T(8,128)(2,1)} fusion(f32[4,1024,1024]{1,2,0:T(8,128)} %get-tuple-element.76, f32[4,1024,1024]{1,2,0:T(8,128)S(1)} %bitcast.129, f32[4,1024]{1,0:T(4,128)S(1)} %get-tuple-element.75, f32[4,1024]{1,0:T(4,128)S(1)} %log_add_fusion), kind=kLoop, calls=%fused_computation | loop fusion | flops 16777216 | bytes 41975808 | tf_op jit(solution)/shard_map/convert_element_type | solution.py:115
  480.3 6.2 fusion.47
  486.6 3.1 fusion.24
  489.9 2.1 add_add_fusion.1
  492.5 46.2 %reduce-scatter.23.cloned.1.call-done = bf16[128,2048]{1,0:T(8,128)(2,1)} async-done(((bf16[1024,2048]{1,0:T(8,128)(2,1)}), bf16[128,2048]{1,0:T(8,128)(2,1)}) %reduce-scatter.23.cloned.1.call-update) | async-done | bytes 524304 | tf_op jit(solution)/shard_map/reduce_scatter | solution.py:218
  538.9 8.6 %fusion.11 = bf16[4,64,1024]{2,1,0:T(8,128)(2,1)S(1)} fusion(bf16[1024,4,64]{0,2,1:T(8,128)(2,1)S(1)} %bitcast.134, f32[4,1024,1024]{1,2,0:T(8,128)} %get-tuple-element.74, f32[4,1024]{1,0:T(4,128)S(1)} %log_add_fusion), kind=kOutput, calls=%fused_computation.52 | convolution fusion | flops 545521664 | bytes 17842176 | tf_op jit(solution)/shard_map/hqk,qhd->khd/dot_general | solution.py:112
  547.5 3.2 convolution_convert_fusion.4
  550.8 4.6 convolution_convert_fusion.5
  555.5 1.5 collective-permute-start.1
  557.1 8.3 %collective-permute-done.1 = bf16[128,1024]{1,0:T(8,128)(2,1)S(1)} collective-permute-done((bf16[128,1024]{1,0:T(8,128)(2,1)S(1)}, bf16[128,1024]{1,0:T(8,128)(2,1)S(1)}, u32[]{:S(2)}, u32[]{:S(2)}) %collective-permute-start.1) | collective-permute-done | bytes 262176 | tf_op jit(solution)/shard_map/ppermute | solution.py:77
  566.8 43.6 %reduce-scatter.27.cloned.1.call-done = bf16[128,1024]{1,0:T(8,128)(2,1)} async-done(((bf16[1024,1024]{1,0:T(8,128)(2,1)}), bf16[128,1024]{1,0:T(8,128)(2,1)}) %reduce-scatter.27.cloned.1.call-update) | async-done | bytes 262160
  611.6 7.2 all_gather.51
  620.1 40.8 %all-reduce.4 = (f32[1024]{0:T(1024)}, f32[1024]{0:T(1024)}, f32[4096]{0:T(1024)}, f32[4096]{0:T(1024)}, f32[1024]{0:T(1024)}) all-reduce(f32[1024]{0:T(1024)S(1)} %dynamic_update_slice.9, f32[1024]{0:T(1024)S(1)} %copy-done.44, f32[4096]{0:T(1024)S(1)} %dynamic_update_slice.10, ...), channel_id=1, replica_groups=mesh['fsdp'=4,'ctx'=2,'tp'=4] {'fsdp','ctx','tp'}, use_global_device_ids=true, to_apply=%region_23.24 | all-reduce | flops 11264 | bytes 90112 | tf_op jit(solution)/shard_map/psum | solution.py:246
  660.8 14.6 %reduce-scatter.25.cloned.1.call-done = bf16[128,256]{1,0:T(8,128)(2,1)} async-done(((bf16[1024,256]{1,0:T(8,128)(2,1)}), bf16[128,256]{1,0:T(8,128)(2,1)}) %reduce-scatter.25.cloned.1.call-update) | async-done | bytes 65552
  676.4 5.0 all_gather.49
  682.1 15.1 %all-gather.23.cloned.1.call-done = bf16[256,2048]{1,0:T(8,128)(2,1)} async-done(((bf16[128,2048]{1,0:T(8,128)(2,1)}), bf16[256,2048]{1,0:T(8,128)(2,1)}) %all-gather.23.cloned.1.call-update) | async-done | bytes 1048592 | tf_op jit(solution)/shard_map/all_gather | solution.py:221
  697.2 2.8 fusion.51
  700.0 30.8 %reduce-scatter.19.cloned.1.call-done = bf16[2,128,1024]{2,1,0:T(8,128)(2,1)} async-done(((bf16[2,512,1024]{2,1,0:T(8,128)(2,1)}), bf16[2,128,1024]{2,1,0:T(8,128)(2,1)}) %reduce-scatter.19.cloned.1.call-update) | async-done | bytes 524304 | tf_op jit(solution)/shard_map/reduce_scatter | solution.py:59
  732.1 1.5 collective-permute-start.3
  733.6 66.1 %reduce-scatter.21.cloned.1.call-done = bf16[128,768]{1,0:T(8,128)(2,1)} async-done(((bf16[1024,768]{1,0:T(8,128)(2,1)}), bf16[128,768]{1,0:T(8,128)(2,1)}) %reduce-scatter.21.cloned.1.call-update) | async-done | bytes 196624 | tf_op jit(solution)/shard_map/reduce_scatter | solution.py:218
  799.7 6.5 all_gather.48
  (217 shorter events, 32.1 us)
Async XLA Ops:
  7.2 14.3 %copy-start.55 = (f32[256]{0:T(256)S(1)}, f32[256]{0:T(256)}, u32[]{:S(2)}) copy-start(f32[256]{0:T(256)} %param.21) | copy-start | bytes 3076
  7.2 14.4 %copy-start.51 = (s32[2,512]{1,0:T(2,128)S(1)}, s32[2,512]{1,0:T(2,128)}, u32[]{:S(2)}) copy-start(s32[2,512]{1,0:T(2,128)} %param.30) | copy-start | bytes 12292
  7.2 18.7 %copy-start.54 = (s32[2,1024]{1,0:T(2,128)S(1)}, s32[2,1024]{1,0:T(2,128)}, u32[]{:S(2)}) copy-start(s32[2,1024]{1,0:T(2,128)} %param.29) | copy-start | bytes 24580
  7.2 18.7 %copy-start.32 = (bf16[256,256]{1,0:T(8,128)(2,1)S(1)}, bf16[256,256]{1,0:T(8,128)(2,1)}, u32[]{:S(2)}) copy-start(bf16[256,256]{1,0:T(8,128)(2,1)} %param.20) | copy-start | bytes 393220
  7.2 51.2 %all-gather.11.cloned.1.call-start = ((), (), s32[]{:S(2)}) async-start(), calls=%async_computation.9 | async-start | bytes 1966080 | tf_op jit(solution)/shard_map/all_gather | solution.py:151
  9.1 72.9 %all-gather.9.cloned.1.call-start = ((), (), s32[]{:S(2)}) async-start(), calls=%async_computation.8 | async-start | bytes 2621440 | tf_op jit(solution)/shard_map/all_gather | solution.py:55
  10.2 9.3 %collective-permute-start = (bf16[128,1024]{1,0:T(8,128)(2,1)S(1)}, bf16[128,1024]{1,0:T(8,128)(2,1)S(1)}, u32[]{:S(2)}, u32[]{:S(2)}) collective-permute-start(bf16[128,1024]{1,0:T(8,128)(2,1)S(1)} %dynamic-slice_bitcast_fusion.3), channel_id=1, source_target_pairs={{0,4},{4,0},{1,5},{5,1},{2,6},{6,2},{3,7},{7,3},{8,12},{12,8},{9,1... | collective-permute-start | bytes 786440 | tf_op jit(solution)/shard_map/ppermute | solution.py:77
  20.5 316.0 %copy-start.5 = (bf16[1,128,1024]{2,1,0:T(8,128)(2,1)}, bf16[1,128,1024]{2,1,0:T(8,128)(2,1)S(1)}, u32[]{:S(2)}) copy-start(bf16[1,128,1024]{2,1,0:T(8,128)(2,1)S(1)} %get-tuple-element.55) | copy-start | bytes 786436
  21.4 124.8 %reduce-scatter.13.cloned.1.call-start = ((), (), s32[]{:S(2)}) async-start(), calls=%async_computation.10 | async-start | bytes 2621440 | tf_op jit(solution)/shard_map/reduce_scatter | solution.py:59
  21.6 65.9 %copy-start.33 = (f32[4,64]{1,0:T(4,128)}, f32[4,64]{1,0:T(4,128)S(1)}, u32[]{:S(2)}) copy-start(f32[4,64]{1,0:T(4,128)S(1)} %mul.511) | copy-start | bytes 3076
  49.2 63.5 %copy-start.15 = (bf16[256,1024]{1,0:T(8,128)(2,1)}, bf16[256,1024]{1,0:T(8,128)(2,1)S(1)}, u32[]{:S(2)}) copy-start(bf16[256,1024]{1,0:T(8,128)(2,1)S(1)} %all_gather.42) | copy-start | bytes 1572868
  49.8 36.4 %copy-start.19 = (f32[1024,32]{0,1:T(8,128)}, f32[1024,32]{0,1:T(8,128)S(1)}, u32[]{:S(2)}) copy-start(f32[1024,32]{0,1:T(8,128)S(1)} %get-tuple-element.66) | copy-start | bytes 393220
  86.0 17.2 %copy-start.14 = (bf16[1024,256]{0,1:T(8,128)(2,1)}, bf16[1024,256]{0,1:T(8,128)(2,1)S(1)}, u32[]{:S(2)}) copy-start(bf16[1024,256]{0,1:T(8,128)(2,1)S(1)} %split.60) | copy-start | bytes 1572868
  86.5 8.6 %copy-start.2 = (f32[1024,4,32]{0,2,1:T(8,128)}, f32[1024,4,32]{0,2,1:T(8,128)S(1)}, u32[]{:S(2)}) copy-start(f32[1024,4,32]{0,2,1:T(8,128)S(1)} %get-tuple-element.64) | copy-start | bytes 1572868
  86.7 8.5 %copy-start.22 = (f32[1024,4]{0,1:T(4,128)}, f32[1024,4]{0,1:T(4,128)S(1)}, u32[]{:S(2)}) copy-start(f32[1024,4]{0,1:T(4,128)S(1)} %fusion.38) | copy-start | bytes 49156
  87.4 7.7 copy-start.28
  95.2 8.0 copy-start.35
  103.2 8.2 %copy-start.37 = (f32[4,1024]{1,0:T(4,128)}, f32[4,1024]{1,0:T(4,128)S(1)}, u32[]{:S(2)}) copy-start(f32[4,1024]{1,0:T(4,128)S(1)} %fusion) | copy-start | bytes 49156
  112.8 35.3 %copy-start.25 = (f32[1024]{0:T(1024)S(1)}, f32[1024]{0:T(1024)}, u32[]{:S(2)}) copy-start(f32[1024]{0:T(1024)} %param.22) | copy-start | bytes 12292
  114.9 114.1 %all-gather.15.cloned.1.call-start = ((), (), s32[]{:S(2)}) async-start(), calls=%async_computation.12 | async-start | bytes 5242880 | tf_op jit(solution)/shard_map/all_gather | solution.py:154
  117.2 134.8 %all-gather.13.cloned.1.call-start = ((), (), s32[]{:S(2)}) async-start(), calls=%async_computation.11 | async-start | bytes 2621440 | tf_op jit(solution)/shard_map/all_gather | solution.py:55
  148.1 111.0 %copy-start.39 = (f32[2,128]{1,0:T(2,128)}, f32[2,128]{1,0:T(2,128)S(1)}, u32[]{:S(2)}) copy-start(f32[2,128]{1,0:T(2,128)S(1)} %fusion.39) | copy-start | bytes 3076
  149.6 102.5 %copy-start.49 = (f32[2,128]{1,0:T(2,128)}, f32[2,128]{1,0:T(2,128)S(1)}, u32[]{:S(2)}) copy-start(f32[2,128]{1,0:T(2,128)S(1)} %multiply_reduce_fusion.7) | copy-start | bytes 3076
  149.6 109.5 %copy-start.41 = (f32[2,128]{1,0:T(2,128)}, f32[2,128]{1,0:T(2,128)S(1)}, u32[]{:S(2)}) copy-start(f32[2,128]{1,0:T(2,128)S(1)} %fusion.40) | copy-start | bytes 3076
  151.9 147.9 %all-gather.17.cloned.1.call-start = ((), (), s32[]{:S(2)}) async-start(), calls=%async_computation.13 | async-start | bytes 2621440 | tf_op jit(solution)/shard_map/all_gather | solution.py:155
  152.5 182.8 %reduce-scatter.15.cloned.1.call-start = ((), (), s32[]{:S(2)}) async-start(), calls=%async_computation.14 | async-start | bytes 2621440 | tf_op jit(solution)/shard_map/reduce_scatter | solution.py:59
  252.1 10.3 %copy-start.45 = (f32[1024]{0:T(1024)S(1)}, f32[1024]{0:T(1024)}, u32[]{:S(2)}) copy-start(f32[1024]{0:T(1024)} %param.27) | copy-start | bytes 12292
  252.1 10.3 %copy-start.50 = (f32[1024]{0:T(1024)S(1)}, f32[1024]{0:T(1024)}, u32[]{:S(2)}) copy-start(f32[1024]{0:T(1024)} %param.26) | copy-start | bytes 12292
  264.7 41.1 %copy-start.24 = (bf16[2,128,1024]{2,1,0:T(8,128)(2,1)S(1)}, bf16[2,128,1024]{2,1,0:T(8,128)(2,1)}, u32[]{:S(2)}) copy-start(bf16[2,128,1024]{2,1,0:T(8,128)(2,1)} %param.31) | copy-start | bytes 1572868
  305.7 30.9 %copy-start.1 = (bf16[2,128,1024]{2,1,0:T(8,128)(2,1)S(1)}, bf16[2,128,1024]{2,1,0:T(8,128)(2,1)}, u32[]{:S(2)}) copy-start(bf16[2,128,1024]{2,1,0:T(8,128)(2,1)} %reduce-scatter.13.cloned.1.call-done) | copy-start | bytes 1572868
  305.7 59.8 %all-gather.19.cloned.1.call-start = ((), (), s32[]{:S(2)}) async-start(), calls=%async_computation.15 | async-start | bytes 2621440 | tf_op jit(solution)/shard_map/all_gather | solution.py:55
  305.8 7.9 collective-permute-start.2
  314.7 23.8 %copy-start.10 = (bf16[1,128,1024]{2,1,0:T(8,128)(2,1)}, bf16[1,128,1024]{2,1,0:T(8,128)(2,1)S(1)}, u32[]{:S(2)}) copy-start(bf16[1,128,1024]{2,1,0:T(8,128)(2,1)S(1)} %get-tuple-element.56) | copy-start | bytes 786436
  314.7 23.8 %copy-start.11 = (bf16[1,128,1024]{2,1,0:T(8,128)(2,1)}, bf16[1,128,1024]{2,1,0:T(8,128)(2,1)S(1)}, u32[]{:S(2)}) copy-start(bf16[1,128,1024]{2,1,0:T(8,128)(2,1)S(1)} %get-tuple-element.57) | copy-start | bytes 786436
  342.8 72.9 %reduce-scatter.17.cloned.1.call-start = ((), (), s32[]{:S(2)}) async-start(), calls=%async_computation.16 | async-start | bytes 2621440 | tf_op jit(solution)/shard_map/reduce_scatter | solution.py:59
  365.5 9.4 %copy-start.46 = (f32[1024]{0:T(1024)S(1)}, f32[1024]{0:T(1024)}, u32[]{:S(2)}) copy-start(f32[1024]{0:T(1024)} %param.27) | copy-start | bytes 12292
  374.9 9.5 %copy-start.59 = (bf16[1024,1024]{1,0:T(8,128)(2,1)}, bf16[1024,1024]{1,0:T(8,128)(2,1)S(1)}, u32[]{:S(2)}) copy-start(bf16[1024,1024]{1,0:T(8,128)(2,1)S(1)} %get-tuple-element.36) | copy-start | bytes 6291460
  375.5 8.9 %copy-start.18 = (bf16[1024,1024]{1,0:T(8,128)(2,1)}, bf16[1024,1024]{1,0:T(8,128)(2,1)S(1)}, u32[]{:S(2)}) copy-start(bf16[1024,1024]{1,0:T(8,128)(2,1)S(1)} %multiply_convert_fusion.1) | copy-start | bytes 6291460
  384.4 62.3 %all-gather.21.cloned.1.call-start = ((), (), s32[]{:S(2)}) async-start(), calls=%async_computation.17 | async-start | bytes 2621440 | tf_op jit(solution)/shard_map/all_gather | solution.py:55
  415.7 7.2 copy-start.26
  415.7 7.2 copy-start.40
  424.0 114.7 %reduce-scatter.23.cloned.1.call-start = ((), (), s32[]{:S(2)}) async-start(), calls=%async_computation.20 | async-start | bytes 4718592 | tf_op jit(solution)/shard_map/reduce_scatter | solution.py:218
  433.5 176.9 %reduce-scatter.27.cloned.1.call-start = ((), (), s32[]{:S(2)}) async-start(), calls=%async_computation.23 | async-start | bytes 2359296
  440.1 6.6 copy-start.16
  444.2 231.3 %reduce-scatter.25.cloned.1.call-start = ((), (), s32[]{:S(2)}) async-start(), calls=%async_computation.22 | async-start | bytes 589824
  449.2 16.7 %copy-start.12 = (bf16[1024,256]{0,1:T(8,128)(2,1)}, bf16[1024,256]{0,1:T(8,128)(2,1)S(1)}, u32[]{:S(2)}) copy-start(bf16[1024,256]{0,1:T(8,128)(2,1)S(1)} %convolution_convert_fusion.7) | copy-start | bytes 1572868
  452.2 13.7 %slice-start = ((s8[16777216]{0:T(1024)(128)(4,1)}), s8[4194304]{0:T(1024)(128)(4,1)S(1)}, s32[]{:S(2)}) async-start(s8[16777216]{0:T(1024)(128)(4,1)} %bitcast.128), calls=%async_computation.24 | async-start | bytes 8388608
  452.2 14.8 %slice-start.1 = ((s8[16777216]{0:T(1024)(128)(4,1)}), s8[4194304]{0:T(1024)(128)(4,1)S(1)}, s32[]{:S(2)}) async-start(s8[16777216]{0:T(1024)(128)(4,1)} %bitcast.128), calls=%async_computation.25 | async-start | bytes 8388608
  452.2 16.0 %slice-start.2 = ((s8[16777216]{0:T(1024)(128)(4,1)}), s8[4194304]{0:T(1024)(128)(4,1)S(1)}, s32[]{:S(2)}) async-start(s8[16777216]{0:T(1024)(128)(4,1)} %bitcast.128), calls=%async_computation.26 | async-start | bytes 8388608
  452.2 17.3 %slice-start.3 = ((s8[16777216]{0:T(1024)(128)(4,1)}), s8[4194304]{0:T(1024)(128)(4,1)S(1)}, s32[]{:S(2)}) async-start(s8[16777216]{0:T(1024)(128)(4,1)} %bitcast.128), calls=%async_computation.27 | async-start | bytes 8388608
  469.5 10.9 %copy-start.3 = (f32[1024,4,32]{0,2,1:T(8,128)S(1)}, f32[1024,4,32]{0,2,1:T(8,128)}, u32[]{:S(2)}) copy-start(f32[1024,4,32]{0,2,1:T(8,128)} %copy-done.2) | copy-start | bytes 1572868
  489.8 207.4 %all-gather.23.cloned.1.call-start = ((), (), s32[]{:S(2)}) async-start(), calls=%async_computation.21 | async-start | bytes 1572864 | tf_op jit(solution)/shard_map/all_gather | solution.py:221
  492.0 46.9 %copy-start.13 = (bf16[1024,256]{0,1:T(8,128)(2,1)S(1)}, bf16[1024,256]{0,1:T(8,128)(2,1)}, u32[]{:S(2)}) copy-start(bf16[1024,256]{0,1:T(8,128)(2,1)} %copy-done.12) | copy-start | bytes 1572868
  538.7 192.1 %reduce-scatter.19.cloned.1.call-start = ((), (), s32[]{:S(2)}) async-start(), calls=%async_computation.18 | async-start | bytes 2621440 | tf_op jit(solution)/shard_map/reduce_scatter | solution.py:59
  538.9 8.6 %copy-start.58 = (bf16[1024,768]{1,0:T(8,128)(2,1)S(1)}, bf16[1024,768]{1,0:T(8,128)(2,1)}, u32[]{:S(2)}) copy-start(bf16[1024,768]{1,0:T(8,128)(2,1)} %all-gather.11.cloned.1.call-done) | copy-start | bytes 4718596
  550.7 248.9 %reduce-scatter.21.cloned.1.call-start = ((), (), s32[]{:S(2)}) async-start(), calls=%async_computation.19 | async-start | bytes 1769472 | tf_op jit(solution)/shard_map/reduce_scatter | solution.py:218
  555.4 10.8 %copy-start.53 = (f32[1024]{0:T(1024)S(1)}, f32[1024]{0:T(1024)}, u32[]{:S(2)}) copy-start(f32[1024]{0:T(1024)} %get-tuple-element.14) | copy-start | bytes 12292
  555.4 11.1 %copy-start.52 = (f32[1024]{0:T(1024)S(1)}, f32[1024]{0:T(1024)}, u32[]{:S(2)}) copy-start(f32[1024]{0:T(1024)} %get-tuple-element.15) | copy-start | bytes 12292
  555.4 64.6 %copy-start.43 = (f32[1024]{0:T(1024)S(1)}, f32[1024]{0:T(1024)}, u32[]{:S(2)}) copy-start(f32[1024]{0:T(1024)} %get-tuple-element.16) | copy-start | bytes 12292
  555.4 64.6 %copy-start.44 = (f32[1024]{0:T(1024)S(1)}, f32[1024]{0:T(1024)}, u32[]{:S(2)}) copy-start(f32[1024]{0:T(1024)} %get-tuple-element.22) | copy-start | bytes 12292
  555.5 9.8 %collective-permute-start.1 = (bf16[128,1024]{1,0:T(8,128)(2,1)S(1)}, bf16[128,1024]{1,0:T(8,128)(2,1)S(1)}, u32[]{:S(2)}, u32[]{:S(2)}) collective-permute-start(bf16[128,1024]{1,0:T(8,128)(2,1)S(1)} %dynamic-slice_bitcast_fusion.2), channel_id=1, source_target_pairs={{0,4},{4,0},{1,5},{5,1},{2,6},{6,2},{3,7},{7,3},{8,12},{12,8},{9,1... | collective-permute-start | bytes 786440 | tf_op jit(solution)/shard_map/ppermute | solution.py:77
  566.2 164.6 %copy-start.7 = (f32[2,128,1024]{2,1,0:T(8,128)S(1)}, f32[2,128,1024]{2,1,0:T(8,128)}, u32[]{:S(2)}) copy-start(f32[2,128,1024]{2,1,0:T(8,128)} %copy-done.6) | copy-start | bytes 3145732
  566.2 164.6 %copy-start.27 = (f32[1024]{0:T(1024)S(1)}, f32[1024]{0:T(1024)}, u32[]{:S(2)}) copy-start(f32[1024]{0:T(1024)} %param.22) | copy-start | bytes 12292
  732.1 75.1 %collective-permute-start.3 = (bf16[128,1024]{1,0:T(8,128)(2,1)S(1)}, bf16[128,1024]{1,0:T(8,128)(2,1)S(1)}, u32[]{:S(2)}, u32[]{:S(2)}) collective-permute-start(bf16[128,1024]{1,0:T(8,128)(2,1)S(1)} %dynamic-slice_bitcast_fusion), channel_id=1, source_target_pairs={{0,4},{4,0},{1,5},{5,1},{2,6},{6,2},{3,7},{7,3},{8,12},{12,8},{9,1... | collective-permute-start | bytes 786440 | tf_op jit(solution)/shard_map/ppermute | solution.py:77
  (20 other events, 60.6 us)
Sparse Core Ops, SparseCore 0:
  10.2 48.1 all-gather.10
  60.5 21.4 all-gather.8
  115.0 31.1 reduce-scatter.12
  148.2 80.7 all-gather.14
  231.0 21.0 all-gather.12
  253.5 46.2 all-gather.16
  305.8 29.3 reduce-scatter.14
  342.9 22.5 all-gather.18
  384.5 31.1 reduce-scatter.16
  424.1 22.5 all-gather.20
  450.3 88.2 reduce-scatter.22
  542.1 68.3 reduce-scatter.26
  613.8 61.6 reduce-scatter.24
  676.8 20.3 all-gather.22
  699.6 31.1 reduce-scatter.18
  734.1 65.5 reduce-scatter.20
where the time goes:
time: 824 us; the launch traced here: 815 us
  waiting for transfers between devices  509 us (62%)
  matrix products  109 us (13%)
  blocking collectives  87.1 us (11%)
  other arithmetic  58.8 us (7%)
  local copies, waits for them, and re-layouts  26.9 us (3%)
  between operations  14.9 us (2%)
  starting transfers between devices  9.26 us (1%)
    reduce_scatter x2, waiting for transfers between devices, sum_rows(): lax.psum_scatter(part.astype(BF), ('fsdp', 'ctx'), scatter_dimension=0, t...  112 us
    reduce_scatter x4, waiting for transfers between devices, reduce_rows(): lax.psum_scatter(values.astype(BF), 'tp', scatter_dimension=1, tiled=True)  111 us
    all_gather x1, waiting for transfers between devices, run(): full_ug = lax.all_gather(ug_shard, 'fsdp', axis=0, tiled=True)  76.5 us
    all_gather x4, waiting for transfers between devices, gather_rows(): return lax.all_gather(values, 'tp', axis=1, tiled=True)  71.6 us
    unnamed x18, waiting for transfers between devices  59 us
    psum x1, blocking collectives, run(): lax.psum((spread_slice(sharp_query + sharp_key), spread_slice(grad_amplit...  40.8 us
    all_gather x1, waiting for transfers between devices, run(): full_down = lax.all_gather(down_weight, 'fsdp', axis=1, tiled=True)  35.1 us
    all_gather x1, blocking collectives, run(): full_output = lax.all_gather(output_weight, 'fsdp', axis=1, tiled=True)  23.3 us
  transfers between devices with their start and end apart: 20, of which 19 were waited for; matrix products, arithmetic and copies ran while one was open for 14% of the time, Pallas kernels for 0%

commit v1 on v0

--- a/solution.py
+++ b/solution.py
@@ -9,6 +9,21 @@
 rope_base = 10000.0
 BF = jnp.bfloat16
 F32 = jnp.float32
+
+
+def state_the_spot(x_part, dev_axis):
+    dev_count = lax.axis_size(dev_axis)
+    line_up = tuple(((no, (no + 1) % dev_count) for no in range(dev_count)))
+    entries = tuple(((no, (no - 1) % dev_count) for no in range(dev_count)))
+    a_next, odd = ([x_part], [x_part])
+    for _ in range(dev_count // 2):
+        a_next.append(lax.ppermute(a_next[-1], dev_axis, perm=line_up))
+    for _ in [*range((dev_count - 1) // 2)]:
+        view_out = lax.ppermute(odd[-1], axis_name=dev_axis, perm=entries)
+        odd.append(view_out)
+    w1 = jnp.concatenate([*a_next[::-1], *odd[1:]], axis=1)
+    mat_out = jnp.roll(w1, (lax.axis_index(dev_axis) - dev_count // 2) * x_part.shape[1], axis=1)
+    return mat_out
 
 
 def unit_rows(values):
@@ -52,7 +67,7 @@
 
 
 def gather_rows(values):
-    return lax.all_gather(values, "tp", axis=1, tiled=True)
+    return state_the_spot(values, "tp")
 
 
 def reduce_rows(values):

time: 824 us -> 757 us (0.919)
  waiting for transfers between devices: 509 us -> 422 us
  other arithmetic: 58.8 us -> 88.6 us
  matrix products: 109 us -> 97.1 us
    all_gather x4 -> x0, waiting for transfers between devices: 71.6 us -> none  [gather_rows(): return lax.all_gather(values, 'tp', axis=1, tiled=True)]
    ppermute x0 -> x12, waiting for transfers between devices: none -> 65.1 us  [the longest x8 55.1 us: state_the_spot(): a_next.append(lax.ppermute(a_next[-1], dev_axis, perm=line_up))]
    reduce_scatter x2, waiting for transfers between devices: 112 us -> 63.9 us  [sum_rows(): lax.psum_scatter(part.astype(BF), ('fsdp', 'ctx'), scatter_dimension=0, t...]
    concatenate x0 -> x4, other arithmetic: none -> 33.6 us  [state_the_spot(): jnp.roll(w1, (lax.axis_index(dev_axis) - dev_count // 2) * x_part.shape[1...]
    all_gather x1, waiting for transfers between devices: 76.5 us -> 46.6 us  [run(): full_ug = lax.all_gather(ug_shard, 'fsdp', axis=0, tiled=True)]
    unnamed x18 -> x14, waiting for transfers between devices: 59 us -> 81.7 us
    reduce_scatter x4, waiting for transfers between devices: 111 us -> 96.9 us  [reduce_rows(): lax.psum_scatter(values.astype(BF), 'tp', scatter_dimension=1, tiled=True)]
    unnamed x132 -> x134, local copies, waits for them, and re-layouts: 19.6 us -> 15.5 us
  transfers between devices with their start and end apart: 20 -> 28, of which waited for: 19 -> 22; matrix products, arithmetic and copies ran while one was open for 14% -> 17% of each run, Pallas kernels for 0% -> 0%
where the time goes in v1:
time: 757 us; the launch traced here: 747 us
  waiting for transfers between devices  422 us (56%)
  matrix products  97.1 us (13%)
  other arithmetic  88.6 us (12%)
  blocking collectives  87.4 us (12%)
  local copies, waits for them, and re-layouts  21.7 us (3%)
  between operations  15.4 us (2%)
  starting transfers between devices  15 us (2%)
    reduce_scatter x4, waiting for transfers between devices, reduce_rows(): lax.psum_scatter(values.astype(BF), 'tp', scatter_dimension=1, tiled=True)  96.9 us
    unnamed x14, waiting for transfers between devices  81.7 us
    reduce_scatter x2, waiting for transfers between devices, sum_rows(): lax.psum_scatter(part.astype(BF), ('fsdp', 'ctx'), scatter_dimension=0, t...  63.9 us
    ppermute x8, waiting for transfers between devices, state_the_spot(): a_next.append(lax.ppermute(a_next[-1], dev_axis, perm=line_up))  55.1 us
    all_gather x1, waiting for transfers between devices, run(): full_ug = lax.all_gather(ug_shard, 'fsdp', axis=0, tiled=True)  46.6 us
    psum x1, blocking collectives, run(): lax.psum((spread_slice(sharp_query + sharp_key), spread_slice(grad_amplit...  40.7 us
    concatenate x4, other arithmetic, state_the_spot(): jnp.roll(w1, (lax.axis_index(dev_axis) - dev_count // 2) * x_part.shape[1...  33.6 us
    all_gather x1, waiting for transfers between devices, run(): full_down = lax.all_gather(down_weight, 'fsdp', axis=1, tiled=True)  33.6 us
  transfers between devices with their start and end apart: 28, of which 22 were waited for; matrix products, arithmetic and copies ran while one was open for 17% of the time, Pallas kernels for 0%

profile of v1, /device:TPU:0, one launch (start us, length us, event | category | flops | bytes accessed | tf_op | source)
XLA Modules:
  0.0 746.8 jit_solution(10174493325256648285)
XLA Ops:
  8.2 3.0 collective-permute-start
  11.2 1.8 pad_maximum_fusion.14
  13.1 4.4 collective-permute-done
  19.4 4.5 all_gather.28
  24.6 23.5 %all_gather.29 = bf16[256,1024]{1,0:T(8,128)(2,1)S(1)} all-gather(bf16[256,256]{1,0:T(8,128)(2,1)} %param.22), channel_id=1, replica_groups=mesh['fsdp'=4,'ctx'=2,'tp'=4] {'fsdp'}, dimensions={1}, use_global_device_ids=true | all-gather | bytes 655360 | tf_op jit(solution)/shard_map/all_gather | solution.py:167
  49.9 10.1 %collective-permute-done.3 = bf16[2,128,1024]{2,1,0:T(8,128)(2,1)S(1)} collective-permute-done((bf16[2,128,1024]{2,1,0:T(8,128)(2,1)}, bf16[2,128,1024]{2,1,0:T(8,128)(2,1)S(1)}, u32[]{:S(2)}, u32[]{:S(2)}) %collective-permute-start.3) | collective-permute-done | bytes 524320 | tf_op jit(solution)/shard_map/ppermute | solution.py:22
  60.0 2.3 collective-permute-done.2
  62.3 8.3 %fusion.34 = bf16[2,512,1024]{2,1,0:T(8,128)(2,1)} fusion(s32[]{:T(128)S(6)} %select_n.95, bf16[2,128,1024]{2,1,0:T(8,128)(2,1)} %collective-permute-done.2, bf16[2,128,1024]{2,1,0:T(8,128)(2,1)S(1)} %collective-permute-done.1, bf16[1,128,1024]{2,1,0:T(8,128)(2,1)S(1)} %get-tuple-element.55, bf16[1,128,1024]{2,1,0:T(8,128)(2,1)S(1)} %get-tuple-element.56, ...), kind=kLoop, calls=%fused_computation.84 | loop fusion | flops 20971520 | bytes 4194308 | tf_op jit(solution)/shard_map/jit(_roll_dynamic)/concatenate | solution.py:25
  70.6 3.9 fusion.85
  75.5 7.6 %fusion.84 = (f32[4,1024]{1,0:T(4,128)S(1)}, f32[4,1024,1024]{1,2,0:T(8,128)}) fusion(f32[1024,4]{0,1:T(4,128)S(1)} %fusion.68, f32[4,64]{1,0:T(4,128)S(1)} %mul.518, f32[1024,4,32]{0,2,1:T(8,128)S(1)} %get-tuple-element.45, f32[1024,4,32]{0,2,1:T(8,128)S(1)} %get-tuple-element.44, f32[1024,4]{0,1:T(4,128)S(1)} %fusion.67, ...), kind=kOutput, calls=%fused_computation.228 | convolution fusion | flops 551546880 | bytes 19973120 | tf_op jit(solution)/shard_map/qhd,khd->hqk/dot_general | solution.py:105
  83.1 8.0 %fusion = f32[4,1024]{1,0:T(4,128)S(1)} fusion(f32[4,1024,1024]{1,2,0:T(8,128)} %get-tuple-element.75, f32[4,1024]{1,0:T(4,128)S(1)} %get-tuple-element.74), kind=kLoop, calls=%fused_computation.6 | loop fusion | flops 8384512 | bytes 16809984 | tf_op jit(solution)/shard_map/reduce_sum | solution.py:110
  91.1 7.8 %fusion.44 = bf16[4,64,1024]{2,1,0:T(8,128)(2,1)S(1)} fusion(bf16[1024,4,64]{0,2,1:T(8,128)(2,1)S(1)} %bitcast.133, f32[4,1024,1024]{1,2,0:T(8,128)} %get-tuple-element.75, f32[4,1024]{1,0:T(4,128)S(1)} %fusion, f32[4,1024]{1,0:T(4,128)S(1)} %get-tuple-element.74), kind=kOutput, calls=%fused_computation.119 | convolution fusion | flops 549715968 | bytes 17858560 | tf_op jit(solution)/shard_map/hqk,khd->qhd/dot_general | solution.py:112
  99.4 2.1 convolution_convert_fusion.3
  101.6 2.3 pad_maximum_fusion.8
  103.9 29.3 %reduce-scatter.13.cloned.1.call-done = bf16[2,128,1024]{2,1,0:T(8,128)(2,1)} async-done(((bf16[2,512,1024]{2,1,0:T(8,128)(2,1)}), bf16[2,128,1024]{2,1,0:T(8,128)(2,1)}) %reduce-scatter.13.cloned.1.call-update) | async-done | bytes 524304 | tf_op jit(solution)/shard_map/reduce_scatter | solution.py:74
  138.2 1.8 collective-permute-start.6
  140.0 11.6 %collective-permute-done.4 = bf16[2,128,1024]{2,1,0:T(8,128)(2,1)S(1)} collective-permute-done((bf16[2,128,1024]{2,1,0:T(8,128)(2,1)S(1)}, bf16[2,128,1024]{2,1,0:T(8,128)(2,1)S(1)}, u32[]{:S(2)}, u32[]{:S(2)}) %collective-permute-start.4) | collective-permute-done | bytes 524320 | tf_op jit(solution)/shard_map/ppermute | solution.py:20
  151.6 8.6 %collective-permute-done.5 = bf16[2,128,1024]{2,1,0:T(8,128)(2,1)S(1)} collective-permute-done((bf16[2,128,1024]{2,1,0:T(8,128)(2,1)S(1)}, bf16[2,128,1024]{2,1,0:T(8,128)(2,1)S(1)}, u32[]{:S(2)}, u32[]{:S(2)}) %collective-permute-start.5) | collective-permute-done | bytes 524320 | tf_op jit(solution)/shard_map/ppermute | solution.py:20
  160.2 9.4 %fusion.27 = bf16[2,512,1024]{2,1,0:T(8,128)(2,1)} fusion(s32[]{:T(128)S(6)} %select_n.95, bf16[2,128,1024]{2,1,0:T(8,128)(2,1)S(1)} %collective-permute-done.5, bf16[2,128,1024]{2,1,0:T(8,128)(2,1)S(1)} %collective-permute-done.4, bf16[2,128,1024]{2,1,0:T(8,128)(2,1)S(1)} %multiply_convert_fusion.7, bf16[2,128,1024]{2,1,0:T(8,128)(2,1)S(1)} %collective-permute-done.6), kind=kLoop, calls=%fused_computation.77 | loop fusion | flops 16777216 | bytes 4194308 | tf_op jit(solution)/shard_map/jit(_roll_dynamic)/concatenate | solution.py:25
  169.5 46.6 %all-gather.7.cloned.1.call-done = bf16[1024,2048]{1,0:T(8,128)(2,1)} async-done(((bf16[256,2048]{1,0:T(8,128)(2,1)}), bf16[1024,2048]{1,0:T(8,128)(2,1)}) %all-gather.7.cloned.1.call-update) | async-done | bytes 4194320 | tf_op jit(solution)/shard_map/all_gather | solution.py:169
  216.2 6.9 fusion.86
  223.2 3.3 copy-done.8
  226.5 2.3 multiply_convert_fusion.3
  228.8 33.6 %all-gather.9.cloned.1.call-done = bf16[1024,1024]{1,0:T(8,128)(2,1)} async-done(((bf16[1024,256]{1,0:T(8,128)(2,1)}), bf16[1024,1024]{1,0:T(8,128)(2,1)}) %all-gather.9.cloned.1.call-update) | async-done | bytes 2097168 | tf_op jit(solution)/shard_map/all_gather | solution.py:170
  262.4 5.9 convolution_convert_fusion.2
  270.1 6.4 collective-permute-done.8
  276.5 21.3 %reduce-scatter.15.cloned.1.call-done = bf16[2,128,1024]{2,1,0:T(8,128)(2,1)} async-done(((bf16[2,512,1024]{2,1,0:T(8,128)(2,1)}), bf16[2,128,1024]{2,1,0:T(8,128)(2,1)}) %reduce-scatter.15.cloned.1.call-update) | async-done | bytes 524304 | tf_op jit(solution)/shard_map/reduce_scatter | solution.py:74
  299.1 1.9 fusion.45
  301.1 2.5 fusion.52
  306.4 11.9 %collective-permute-done.9 = bf16[2,128,1024]{2,1,0:T(8,128)(2,1)S(1)} collective-permute-done((bf16[2,128,1024]{2,1,0:T(8,128)(2,1)S(1)}, bf16[2,128,1024]{2,1,0:T(8,128)(2,1)S(1)}, u32[]{:S(2)}, u32[]{:S(2)}) %collective-permute-start.9) | collective-permute-done | bytes 524320 | tf_op jit(solution)/shard_map/ppermute | solution.py:20
  318.3 8.6 %collective-permute-done.10 = bf16[2,128,1024]{2,1,0:T(8,128)(2,1)S(1)} collective-permute-done((bf16[2,128,1024]{2,1,0:T(8,128)(2,1)S(1)}, bf16[2,128,1024]{2,1,0:T(8,128)(2,1)S(1)}, u32[]{:S(2)}, u32[]{:S(2)}) %collective-permute-start.10) | collective-permute-done | bytes 524320 | tf_op jit(solution)/shard_map/ppermute | solution.py:20
  326.9 8.4 %fusion.20 = bf16[2,512,1024]{2,1,0:T(8,128)(2,1)S(1)} fusion(s32[]{:T(128)S(6)} %select_n.95, bf16[2,128,1024]{2,1,0:T(8,128)(2,1)S(1)} %collective-permute-done.10, bf16[2,128,1024]{2,1,0:T(8,128)(2,1)S(1)} %collective-permute-done.9, bf16[2,128,1024]{2,1,0:T(8,128)(2,1)S(1)} %fusion.46, bf16[2,128,1024]{2,1,0:T(8,128)(2,1)S(1)} %collective-permute-done.11), kind=kLoop, calls=%fused_computation.70 | loop fusion | flops 16777216 | bytes 4194308 | tf_op jit(solution)/shard_map/jit(_roll_dynamic)/concatenate | solution.py:25
  335.4 8.5 %multiply_reduce_fusion.1 = (f32[1024]{0:T(1024)}, f32[1024]{0:T(1024)}, f32[1024,1024]{1,0:T(8,128)S(1)}, bf16[1024,1024]{1,0:T(8,128)(2,1)S(1)}) fusion(f32[1024,2048]{1,0:T(8,128)} %copy-done.8, f32[1024]{0:T(1024)S(1)} %copy-done.50, f32[1024]{0:T(1024)S(1)} %copy-done.58, bf16[1024,1024]{1,0:T(8,128)(2,1)S(1)} %bitcast.140, ...), kind=kOutput, calls=%fused_computation.49 | convolution fusion | flops 2168453120 | bytes 18890752 | tf_op jit(solution)/shard_map/dot_general | solution.py:66
  344.5 3.1 copy-done.62
  347.5 5.7 fusion.40
  353.6 9.5 %convolution_convert_fusion = bf16[1024,2048]{1,0:T(8,128)(2,1)} fusion(bf16[1024,1024]{1,0:T(8,128)(2,1)} %bitcast.139, bf16[1024,1024]{1,0:T(8,128)(2,1)} %copy-done.21, bf16[1024,1024]{1,0:T(8,128)(2,1)} %copy-done.64), kind=kOutput, calls=%fused_computation.58 | convolution fusion | flops 4305453056 | bytes 10485760 | tf_op jit(solution)/shard_map/dot_general | solution.py:62
  363.2 21.2 %reduce-scatter.17.cloned.1.call-done = bf16[2,128,1024]{2,1,0:T(8,128)(2,1)} async-done(((bf16[2,512,1024]{2,1,0:T(8,128)(2,1)}), bf16[2,128,1024]{2,1,0:T(8,128)(2,1)}) %reduce-scatter.17.cloned.1.call-update) | async-done | bytes 524304 | tf_op jit(solution)/shard_map/reduce_scatter | solution.py:74
  384.4 2.2 multiply_reduce_fusion.3
  386.7 2.6 multiply_reduce_fusion.4
  390.3 1.8 collective-permute-start.14
  392.1 11.7 %collective-permute-done.12 = bf16[2,128,1024]{2,1,0:T(8,128)(2,1)S(1)} collective-permute-done((bf16[2,128,1024]{2,1,0:T(8,128)(2,1)S(1)}, bf16[2,128,1024]{2,1,0:T(8,128)(2,1)S(1)}, u32[]{:S(2)}, u32[]{:S(2)}) %collective-permute-start.12) | collective-permute-done | bytes 524320 | tf_op jit(solution)/shard_map/ppermute | solution.py:20
  403.8 3.8 convolution_convert_fusion.1
  407.6 4.0 copy.46
  412.5 7.5 %fusion.13 = bf16[2,512,1024]{2,1,0:T(8,128)(2,1)S(1)} fusion(s32[]{:T(128)S(6)} %select_n.95, bf16[2,128,1024]{2,1,0:T(8,128)(2,1)} %collective-permute-done.13, bf16[2,128,1024]{2,1,0:T(8,128)(2,1)S(1)} %collective-permute-done.12, bf16[2,128,1024]{2,1,0:T(8,128)(2,1)S(1)} %fusion.47, bf16[2,128,1024]{2,1,0:T(8,128)(2,1)} %collective-permute-done.14), kind=kLoop, calls=%fused_computation.63 | loop fusion | flops 16777216 | bytes 4194308 | tf_op jit(solution)/shard_map/jit(_roll_dynamic)/concatenate | solution.py:25
  420.8 11.1 %multiply_reduce_fusion = (f32[4,1024]{1,0:T(4,128)S(1)}, f32[4,1024,1024]{1,2,0:T(8,128)}) fusion(f32[4,1024,1024]{1,2,0:T(8,128)} %get-tuple-element.75, f32[4,1024]{1,0:T(4,128)S(1)} %log_add_fusion, bf16[1024,4,64]{0,2,1:T(8,128)(2,1)S(1)} %bitcast.131, bf16[1024,4,64]{0,2,1:T(8,128)(2,1)S(1)} %bitcast.134), kind=kOutput, calls=%fused_computation.1 | convolution fusion | flops 549449728 | bytes 34635776 | tf_op jit(solution)/shard_map/qhd,khd->hqk/dot_general | solution.py:128
  433.7 12.3 %multiply_convert_fusion = bf16[4,1024,1024]{1,2,0:T(8,128)(2,1)S(1)} fusion(f32[4,1024,1024]{1,2,0:T(8,128)} %get-tuple-element.77, f32[4,1024,1024]{1,2,0:T(8,128)} %get-tuple-element.75, f32[4,1024]{1,0:T(4,128)S(1)} %get-tuple-element.76, f32[4,1024]{1,0:T(4,128)S(1)} %log_add_fusion), kind=kLoop, calls=%fused_computation | loop fusion | flops 16777216 | bytes 41975808 | tf_op jit(solution)/shard_map/convert_element_type | solution.py:130
  446.0 2.7 fusion.78
  448.7 3.6 fusion.54
  452.7 1.8 add_add_fusion.1
  455.5 8.7 %fusion.41 = bf16[4,64,1024]{2,1,0:T(8,128)(2,1)S(1)} fusion(bf16[1024,4,64]{0,2,1:T(8,128)(2,1)S(1)} %bitcast.132, f32[4,1024,1024]{1,2,0:T(8,128)} %get-tuple-element.75, f32[4,1024]{1,0:T(4,128)S(1)} %log_add_fusion), kind=kOutput, calls=%fused_computation.116 | convolution fusion | flops 545521664 | bytes 17842176 | tf_op jit(solution)/shard_map/hqk,qhd->khd/dot_general | solution.py:127
  464.2 3.1 convolution_convert_fusion.5
  467.4 4.6 convolution_convert_fusion.4
  473.6 2.7 reduce-scatter.23.cloned.1.call-done
  476.4 3.2 collective-permute-done.7
  480.9 66.9 %reduce-scatter.27.cloned.1.call-done = bf16[128,1024]{1,0:T(8,128)(2,1)} async-done(((bf16[1024,1024]{1,0:T(8,128)(2,1)}), bf16[128,1024]{1,0:T(8,128)(2,1)}) %reduce-scatter.27.cloned.1.call-update) | async-done | bytes 262160
  549.0 7.3 all_gather.35
  557.6 40.7 %all-reduce.4 = (f32[1024]{0:T(1024)}, f32[1024]{0:T(1024)}, f32[4096]{0:T(1024)}, f32[4096]{0:T(1024)}, f32[1024]{0:T(1024)}) all-reduce(f32[1024]{0:T(1024)S(1)} %dynamic_update_slice.9, f32[1024]{0:T(1024)S(1)} %copy-done.48, f32[4096]{0:T(1024)S(1)} %dynamic_update_slice.10, ...), channel_id=1, replica_groups=mesh['fsdp'=4,'ctx'=2,'tp'=4] {'fsdp','ctx','tp'}, use_global_device_ids=true, to_apply=%region_23.25 | all-reduce | flops 11264 | bytes 90112 | tf_op jit(solution)/shard_map/psum | solution.py:261
  598.2 14.6 %reduce-scatter.25.cloned.1.call-done = bf16[128,256]{1,0:T(8,128)(2,1)} async-done(((bf16[1024,256]{1,0:T(8,128)(2,1)}), bf16[128,256]{1,0:T(8,128)(2,1)}) %reduce-scatter.25.cloned.1.call-update) | async-done | bytes 65552
  613.8 5.0 all_gather.33
  619.5 61.2 %reduce-scatter.21.cloned.1.call-done = bf16[128,768]{1,0:T(8,128)(2,1)} async-done(((bf16[1024,768]{1,0:T(8,128)(2,1)}), bf16[128,768]{1,0:T(8,128)(2,1)}) %reduce-scatter.21.cloned.1.call-update) | async-done | bytes 196624 | tf_op jit(solution)/shard_map/reduce_scatter | solution.py:233
  680.7 6.5 all_gather.32
  688.1 25.1 %reduce-scatter.19.cloned.1.call-done = bf16[2,128,1024]{2,1,0:T(8,128)(2,1)} async-done(((bf16[2,512,1024]{2,1,0:T(8,128)(2,1)}), bf16[2,128,1024]{2,1,0:T(8,128)(2,1)}) %reduce-scatter.19.cloned.1.call-update) | async-done | bytes 524304 | tf_op jit(solution)/shard_map/reduce_scatter | solution.py:74
  716.0 19.9 %all-gather.11.cloned.1.call-done = bf16[256,2048]{1,0:T(8,128)(2,1)} async-done(((bf16[128,2048]{1,0:T(8,128)(2,1)}), bf16[256,2048]{1,0:T(8,128)(2,1)}) %all-gather.11.cloned.1.call-update) | async-done | bytes 1048592 | tf_op jit(solution)/shard_map/all_gather | solution.py:236
  735.9 2.8 fusion.82
  (234 shorter events, 36.3 us)
Async XLA Ops:
  7.2 41.5 %copy-start.61 = (f32[256]{0:T(256)S(1)}, f32[256]{0:T(256)}, u32[]{:S(2)}) copy-start(f32[256]{0:T(256)} %param.23) | copy-start | bytes 3076
  7.2 63.4 %all-gather.5.cloned.1.call-start = ((), (), s32[]{:S(2)}) async-start(), calls=%async_computation.8 | async-start | bytes 1966080 | tf_op jit(solution)/shard_map/all_gather | solution.py:166
  8.2 9.3 %collective-permute-start = (bf16[128,1024]{1,0:T(8,128)(2,1)S(1)}, bf16[128,1024]{1,0:T(8,128)(2,1)S(1)}, u32[]{:S(2)}, u32[]{:S(2)}) collective-permute-start(bf16[128,1024]{1,0:T(8,128)(2,1)S(1)} %dynamic-slice_bitcast_fusion.3), channel_id=1, source_target_pairs={{0,4},{4,0},{1,5},{5,1},{2,6},{6,2},{3,7},{7,3},{8,12},{12,8},{9,1... | collective-permute-start | bytes 786440 | tf_op jit(solution)/shard_map/ppermute | solution.py:92
  13.1 120.2 %reduce-scatter.13.cloned.1.call-start = ((), (), s32[]{:S(2)}) async-start(), calls=%async_computation.9 | async-start | bytes 2621440 | tf_op jit(solution)/shard_map/reduce_scatter | solution.py:74
  19.4 28.7 %collective-permute-start.1 = (bf16[2,128,1024]{2,1,0:T(8,128)(2,1)}, bf16[2,128,1024]{2,1,0:T(8,128)(2,1)S(1)}, u32[]{:S(2)}, u32[]{:S(2)}) collective-permute-start(bf16[2,128,1024]{2,1,0:T(8,128)(2,1)} %pad_maximum_fusion.11), channel_id=1, source_target_pairs={{0,1},{1,2},{2,3},{3,0},{4,5},{5,6},{6,7},{7,4},{8,9},{9,10},{10,1... | collective-permute-start | bytes 1572872 | tf_op jit(solution)/shard_map/ppermute | solution.py:20
  48.1 51.3 %copy-start.17 = (bf16[256,1024]{1,0:T(8,128)(2,1)}, bf16[256,1024]{1,0:T(8,128)(2,1)S(1)}, u32[]{:S(2)}) copy-start(bf16[256,1024]{1,0:T(8,128)(2,1)S(1)} %all_gather.29) | copy-start | bytes 1572868
  48.1 11.9 %collective-permute-start.3 = (bf16[2,128,1024]{2,1,0:T(8,128)(2,1)}, bf16[2,128,1024]{2,1,0:T(8,128)(2,1)S(1)}, u32[]{:S(2)}, u32[]{:S(2)}) collective-permute-start(bf16[2,128,1024]{2,1,0:T(8,128)(2,1)} %pad_maximum_fusion.11), channel_id=1, source_target_pairs={{0,3},{1,0},{2,1},{3,2},{4,7},{5,4},{6,5},{7,6},{8,11},{9,8},{10,9... | collective-permute-start | bytes 1572872 | tf_op jit(solution)/shard_map/ppermute | solution.py:22
  48.1 14.2 %collective-permute-start.2 = (bf16[2,128,1024]{2,1,0:T(8,128)(2,1)S(1)}, bf16[2,128,1024]{2,1,0:T(8,128)(2,1)}, u32[]{:S(2)}, u32[]{:S(2)}) collective-permute-start(bf16[2,128,1024]{2,1,0:T(8,128)(2,1)S(1)} %collective-permute-done.1), channel_id=1, source_target_pairs={{0,1},{1,2},{2,3},{3,0},{4,5},{5,6},{6,7},{7,4},{8,9},{9,10},{10,1... | collective-permute-start | bytes 1572872 | tf_op jit(solution)/shard_map/ppermute | solution.py:20
  48.7 26.7 %copy-start.36 = (f32[4,64]{1,0:T(4,128)}, f32[4,64]{1,0:T(4,128)S(1)}, u32[]{:S(2)}) copy-start(f32[4,64]{1,0:T(4,128)S(1)} %mul.518) | copy-start | bytes 3076
  49.3 25.5 %copy-start.22 = (f32[1024,32]{0,1:T(8,128)}, f32[1024,32]{0,1:T(8,128)S(1)}, u32[]{:S(2)}) copy-start(f32[1024,32]{0,1:T(8,128)S(1)} %get-tuple-element.67) | copy-start | bytes 393220
  74.6 16.5 %copy-start.12 = (bf16[1024,256]{0,1:T(8,128)(2,1)}, bf16[1024,256]{0,1:T(8,128)(2,1)S(1)}, u32[]{:S(2)}) copy-start(bf16[1024,256]{0,1:T(8,128)(2,1)S(1)} %split.60) | copy-start | bytes 1572868
  99.4 35.7 %copy-start.29 = (f32[1024]{0:T(1024)S(1)}, f32[1024]{0:T(1024)}, u32[]{:S(2)}) copy-start(f32[1024]{0:T(1024)} %param.24) | copy-start | bytes 12292
  101.5 114.6 %all-gather.7.cloned.1.call-start = ((), (), s32[]{:S(2)}) async-start(), calls=%async_computation.10 | async-start | bytes 5242880 | tf_op jit(solution)/shard_map/all_gather | solution.py:169
  103.9 158.5 %all-gather.9.cloned.1.call-start = ((), (), s32[]{:S(2)}) async-start(), calls=%async_computation.11 | async-start | bytes 2621440 | tf_op jit(solution)/shard_map/all_gather | solution.py:170
  135.1 88.1 %copy-start.42 = (f32[2,128]{1,0:T(2,128)}, f32[2,128]{1,0:T(2,128)S(1)}, u32[]{:S(2)}) copy-start(f32[2,128]{1,0:T(2,128)S(1)} %fusion.70) | copy-start | bytes 3076
  136.6 79.6 %copy-start.53 = (f32[2,128]{1,0:T(2,128)}, f32[2,128]{1,0:T(2,128)S(1)}, u32[]{:S(2)}) copy-start(f32[2,128]{1,0:T(2,128)S(1)} %multiply_reduce_fusion.7) | copy-start | bytes 3076
  136.6 86.5 %copy-start.44 = (f32[2,128]{1,0:T(2,128)}, f32[2,128]{1,0:T(2,128)S(1)}, u32[]{:S(2)}) copy-start(f32[2,128]{1,0:T(2,128)S(1)} %fusion.71) | copy-start | bytes 3076
  138.1 13.5 %collective-permute-start.4 = (bf16[2,128,1024]{2,1,0:T(8,128)(2,1)S(1)}, bf16[2,128,1024]{2,1,0:T(8,128)(2,1)S(1)}, u32[]{:S(2)}, u32[]{:S(2)}) collective-permute-start(bf16[2,128,1024]{2,1,0:T(8,128)(2,1)S(1)} %multiply_convert_fusion.7), channel_id=1, source_target_pairs={{0,1},{1,2},{2,3},{3,0},{4,5},{5,6},{6,7},{7,4},{8,9},{9,10},{10,1... | collective-permute-start | bytes 1572872 | tf_op jit(solution)/shard_map/ppermute | solution.py:20
  138.2 159.6 %reduce-scatter.15.cloned.1.call-start = ((), (), s32[]{:S(2)}) async-start(), calls=%async_computation.12 | async-start | bytes 2621440 | tf_op jit(solution)/shard_map/reduce_scatter | solution.py:74
  138.2 13.4 %collective-permute-start.6 = (bf16[2,128,1024]{2,1,0:T(8,128)(2,1)S(1)}, bf16[2,128,1024]{2,1,0:T(8,128)(2,1)S(1)}, u32[]{:S(2)}, u32[]{:S(2)}) collective-permute-start(bf16[2,128,1024]{2,1,0:T(8,128)(2,1)S(1)} %multiply_convert_fusion.7), channel_id=1, source_target_pairs={{0,3},{1,0},{2,1},{3,2},{4,7},{5,4},{6,5},{7,6},{8,11},{9,8},{10,9... | collective-permute-start | bytes 1572872 | tf_op jit(solution)/shard_map/ppermute | solution.py:22
  151.6 8.6 %collective-permute-start.5 = (bf16[2,128,1024]{2,1,0:T(8,128)(2,1)S(1)}, bf16[2,128,1024]{2,1,0:T(8,128)(2,1)S(1)}, u32[]{:S(2)}, u32[]{:S(2)}) collective-permute-start(bf16[2,128,1024]{2,1,0:T(8,128)(2,1)S(1)} %collective-permute-done.4), channel_id=1, source_target_pairs={{0,1},{1,2},{2,3},{3,0},{4,5},{5,6},{6,7},{7,4},{8,9},{9,10},{10,1... | collective-permute-start | bytes 1572872 | tf_op jit(solution)/shard_map/ppermute | solution.py:20
  216.2 10.3 %copy-start.57 = (f32[1024]{0:T(1024)S(1)}, f32[1024]{0:T(1024)}, u32[]{:S(2)}) copy-start(f32[1024]{0:T(1024)} %param.28) | copy-start | bytes 12292
  228.8 39.7 %copy-start.26 = (bf16[2,128,1024]{2,1,0:T(8,128)(2,1)S(1)}, bf16[2,128,1024]{2,1,0:T(8,128)(2,1)}, u32[]{:S(2)}) copy-start(bf16[2,128,1024]{2,1,0:T(8,128)(2,1)} %param.33) | copy-start | bytes 1572868
  268.2 30.9 %copy-start = (bf16[2,128,1024]{2,1,0:T(8,128)(2,1)S(1)}, bf16[2,128,1024]{2,1,0:T(8,128)(2,1)}, u32[]{:S(2)}) copy-start(bf16[2,128,1024]{2,1,0:T(8,128)(2,1)} %reduce-scatter.13.cloned.1.call-done) | copy-start | bytes 1572868
  268.3 116.1 %reduce-scatter.17.cloned.1.call-start = ((), (), s32[]{:S(2)}) async-start(), calls=%async_computation.13 | async-start | bytes 2621440 | tf_op jit(solution)/shard_map/reduce_scatter | solution.py:74
  268.5 7.9 %collective-permute-start.8 = (bf16[128,1024]{1,0:T(8,128)(2,1)S(1)}, bf16[128,1024]{1,0:T(8,128)(2,1)S(1)}, u32[]{:S(2)}, u32[]{:S(2)}) collective-permute-start(bf16[128,1024]{1,0:T(8,128)(2,1)S(1)} %dynamic-slice_bitcast_fusion.1), channel_id=1, source_target_pairs={{0,4},{4,0},{1,5},{5,1},{2,6},{6,2},{3,7},{7,3},{8,12},{12,8},{9,1... | collective-permute-start | bytes 786440 | tf_op jit(solution)/shard_map/ppermute | solution.py:92
  276.5 24.6 %copy-start.9 = (bf16[1,128,1024]{2,1,0:T(8,128)(2,1)}, bf16[1,128,1024]{2,1,0:T(8,128)(2,1)S(1)}, u32[]{:S(2)}) copy-start(bf16[1,128,1024]{2,1,0:T(8,128)(2,1)S(1)} %get-tuple-element.58) | copy-start | bytes 786436
  301.1 34.3 %copy-start.50 = (f32[1024]{0:T(1024)S(1)}, f32[1024]{0:T(1024)}, u32[]{:S(2)}) copy-start(f32[1024]{0:T(1024)} %param.29) | copy-start | bytes 12292
  301.1 34.3 %copy-start.58 = (f32[1024]{0:T(1024)S(1)}, f32[1024]{0:T(1024)}, u32[]{:S(2)}) copy-start(f32[1024]{0:T(1024)} %param.28) | copy-start | bytes 12292
  301.1 34.2 %copy-start.63 = (bf16[1024,1024]{1,0:T(8,128)(2,1)S(1)}, bf16[1024,1024]{1,0:T(8,128)(2,1)}, u32[]{:S(2)}) copy-start(bf16[1024,1024]{1,0:T(8,128)(2,1)} %all-gather.9.cloned.1.call-done) | copy-start | bytes 6291460
  304.6 13.7 %collective-permute-start.9 = (bf16[2,128,1024]{2,1,0:T(8,128)(2,1)S(1)}, bf16[2,128,1024]{2,1,0:T(8,128)(2,1)S(1)}, u32[]{:S(2)}, u32[]{:S(2)}) collective-permute-start(bf16[2,128,1024]{2,1,0:T(8,128)(2,1)S(1)} %fusion.46), channel_id=1, source_target_pairs={{0,1},{1,2},{2,3},{3,0},{4,5},{5,6},{6,7},{7,4},{8,9},{9,10},{10,1... | collective-permute-start | bytes 1572872 | tf_op jit(solution)/shard_map/ppermute | solution.py:20
  304.7 13.6 %collective-permute-start.11 = (bf16[2,128,1024]{2,1,0:T(8,128)(2,1)S(1)}, bf16[2,128,1024]{2,1,0:T(8,128)(2,1)S(1)}, u32[]{:S(2)}, u32[]{:S(2)}) collective-permute-start(bf16[2,128,1024]{2,1,0:T(8,128)(2,1)S(1)} %fusion.46), channel_id=1, source_target_pairs={{0,3},{1,0},{2,1},{3,2},{4,7},{5,4},{6,5},{7,6},{8,11},{9,8},{10,9... | collective-permute-start | bytes 1572872 | tf_op jit(solution)/shard_map/ppermute | solution.py:22
  318.3 8.6 %collective-permute-start.10 = (bf16[2,128,1024]{2,1,0:T(8,128)(2,1)S(1)}, bf16[2,128,1024]{2,1,0:T(8,128)(2,1)S(1)}, u32[]{:S(2)}, u32[]{:S(2)}) collective-permute-start(bf16[2,128,1024]{2,1,0:T(8,128)(2,1)S(1)} %collective-permute-done.9), channel_id=1, source_target_pairs={{0,1},{1,2},{2,3},{3,0},{4,5},{5,6},{6,7},{7,4},{8,9},{9,10},{10,1... | collective-permute-start | bytes 1572872 | tf_op jit(solution)/shard_map/ppermute | solution.py:20
  353.3 123.0 %reduce-scatter.23.cloned.1.call-start = ((), (), s32[]{:S(2)}) async-start(), calls=%async_computation.16 | async-start | bytes 4718592 | tf_op jit(solution)/shard_map/reduce_scatter | solution.py:233
  363.1 21.3 %copy-start.30 = (f32[1024]{0:T(1024)S(1)}, f32[1024]{0:T(1024)}, u32[]{:S(2)}) copy-start(f32[1024]{0:T(1024)} %param.24) | copy-start | bytes 12292
  363.1 21.3 %copy-start.35 = (f32[1024]{0:T(1024)S(1)}, f32[1024]{0:T(1024)}, u32[]{:S(2)}) copy-start(f32[1024]{0:T(1024)} %param.30) | copy-start | bytes 12292
  363.1 21.3 %copy-start.43 = (f32[2,128]{1,0:T(2,128)S(1)}, f32[2,128]{1,0:T(2,128)}, u32[]{:S(2)}) copy-start(f32[2,128]{1,0:T(2,128)} %copy-done.42) | copy-start | bytes 3076
  363.1 21.3 %copy-start.45 = (f32[2,128]{1,0:T(2,128)S(1)}, f32[2,128]{1,0:T(2,128)}, u32[]{:S(2)}) copy-start(f32[2,128]{1,0:T(2,128)} %copy-done.44) | copy-start | bytes 3076
  363.1 21.3 %copy-start.47 = (f32[2,128]{1,0:T(2,128)S(1)}, f32[2,128]{1,0:T(2,128)}, u32[]{:S(2)}) copy-start(f32[2,128]{1,0:T(2,128)} %copy-done.46) | copy-start | bytes 3076
  363.1 23.6 %copy-start.54 = (f32[2,128]{1,0:T(2,128)S(1)}, f32[2,128]{1,0:T(2,128)}, u32[]{:S(2)}) copy-start(f32[2,128]{1,0:T(2,128)} %copy-done.53) | copy-start | bytes 3076
  363.1 26.2 %copy-start.52 = (f32[2,128]{1,0:T(2,128)S(1)}, f32[2,128]{1,0:T(2,128)}, u32[]{:S(2)}) copy-start(f32[2,128]{1,0:T(2,128)} %copy-done.51) | copy-start | bytes 3076
  363.1 27.1 %copy-start.37 = (f32[4,64]{1,0:T(4,128)S(1)}, f32[4,64]{1,0:T(4,128)}, u32[]{:S(2)}) copy-start(f32[4,64]{1,0:T(4,128)} %copy-done.36) | copy-start | bytes 3076
  363.1 27.1 %copy-start.39 = (f32[4,1024]{1,0:T(4,128)S(1)}, f32[4,1024]{1,0:T(4,128)}, u32[]{:S(2)}) copy-start(f32[4,1024]{1,0:T(4,128)} %copy-done.38) | copy-start | bytes 49156
  363.2 27.1 %copy-start.41 = (f32[4,1024]{1,0:T(4,128)S(1)}, f32[4,1024]{1,0:T(4,128)}, u32[]{:S(2)}) copy-start(f32[4,1024]{1,0:T(4,128)} %copy-done.40) | copy-start | bytes 49156
  363.2 184.7 %reduce-scatter.27.cloned.1.call-start = ((), (), s32[]{:S(2)}) async-start(), calls=%async_computation.19 | async-start | bytes 2359296
  384.4 19.3 %copy-start.16 = (bf16[2,512,1024]{2,1,0:T(8,128)(2,1)S(1)}, bf16[2,512,1024]{2,1,0:T(8,128)(2,1)}, u32[]{:S(2)}) copy-start(bf16[2,512,1024]{2,1,0:T(8,128)(2,1)} %copy-done.15) | copy-start | bytes 6291460
  384.4 19.3 %copy-start.20 = (bf16[1024,1024]{1,0:T(8,128)(2,1)S(1)}, bf16[1024,1024]{1,0:T(8,128)(2,1)}, u32[]{:S(2)}) copy-start(bf16[1024,1024]{1,0:T(8,128)(2,1)} %multiply_convert_fusion.3) | copy-start | bytes 6291460
  390.2 13.5 %collective-permute-start.12 = (bf16[2,128,1024]{2,1,0:T(8,128)(2,1)S(1)}, bf16[2,128,1024]{2,1,0:T(8,128)(2,1)S(1)}, u32[]{:S(2)}, u32[]{:S(2)}) collective-permute-start(bf16[2,128,1024]{2,1,0:T(8,128)(2,1)S(1)} %fusion.47), channel_id=1, source_target_pairs={{0,1},{1,2},{2,3},{3,0},{4,5},{5,6},{6,7},{7,4},{8,9},{9,10},{10,1... | collective-permute-start | bytes 1572872 | tf_op jit(solution)/shard_map/ppermute | solution.py:20
  390.3 21.7 %collective-permute-start.14 = (bf16[2,128,1024]{2,1,0:T(8,128)(2,1)S(1)}, bf16[2,128,1024]{2,1,0:T(8,128)(2,1)}, u32[]{:S(2)}, u32[]{:S(2)}) collective-permute-start(bf16[2,128,1024]{2,1,0:T(8,128)(2,1)S(1)} %fusion.47), channel_id=1, source_target_pairs={{0,3},{1,0},{2,1},{3,2},{4,7},{5,4},{6,5},{7,6},{8,11},{9,8},{10,9... | collective-permute-start | bytes 1572872 | tf_op jit(solution)/shard_map/ppermute | solution.py:22
  403.7 8.7 %collective-permute-start.13 = (bf16[2,128,1024]{2,1,0:T(8,128)(2,1)S(1)}, bf16[2,128,1024]{2,1,0:T(8,128)(2,1)}, u32[]{:S(2)}, u32[]{:S(2)}) collective-permute-start(bf16[2,128,1024]{2,1,0:T(8,128)(2,1)S(1)} %collective-permute-done.12), channel_id=1, source_target_pairs={{0,1},{1,2},{2,3},{3,0},{4,5},{5,6},{6,7},{7,4},{8,9},{9,10},{10,1... | collective-permute-start | bytes 1572872 | tf_op jit(solution)/shard_map/ppermute | solution.py:20
  411.5 201.3 %reduce-scatter.25.cloned.1.call-start = ((), (), s32[]{:S(2)}) async-start(), calls=%async_computation.18 | async-start | bytes 589824
  420.8 11.2 %copy-start.10 = (bf16[1024,256]{0,1:T(8,128)(2,1)}, bf16[1024,256]{0,1:T(8,128)(2,1)S(1)}, u32[]{:S(2)}) copy-start(bf16[1024,256]{0,1:T(8,128)(2,1)S(1)} %convolution_convert_fusion.7) | copy-start | bytes 1572868
  420.8 11.1 %copy-start.28 = (bf16[4,64,1024]{2,1,0:T(8,128)(2,1)S(1)}, bf16[4,64,1024]{2,1,0:T(8,128)(2,1)}, u32[]{:S(2)}) copy-start(bf16[4,64,1024]{2,1,0:T(8,128)(2,1)} %copy-done.27) | copy-start | bytes 1572868
  433.6 12.4 %copy-start.2 = (f32[1024,4,32]{0,2,1:T(8,128)S(1)}, f32[1024,4,32]{0,2,1:T(8,128)}, u32[]{:S(2)}) copy-start(f32[1024,4,32]{0,2,1:T(8,128)} %copy-done.1) | copy-start | bytes 1572868
  433.7 12.4 %copy-start.4 = (f32[1024,4,32]{0,2,1:T(8,128)S(1)}, f32[1024,4,32]{0,2,1:T(8,128)}, u32[]{:S(2)}) copy-start(f32[1024,4,32]{0,2,1:T(8,128)} %copy-done.3) | copy-start | bytes 1572868
  452.4 228.3 %reduce-scatter.21.cloned.1.call-start = ((), (), s32[]{:S(2)}) async-start(), calls=%async_computation.15 | async-start | bytes 1769472 | tf_op jit(solution)/shard_map/reduce_scatter | solution.py:233
  467.3 245.9 %reduce-scatter.19.cloned.1.call-start = ((), (), s32[]{:S(2)}) async-start(), calls=%async_computation.14 | async-start | bytes 2621440 | tf_op jit(solution)/shard_map/reduce_scatter | solution.py:74
  472.0 85.3 %copy-start.55 = (f32[4,64]{1,0:T(4,128)S(1)}, f32[4,64]{1,0:T(4,128)}, u32[]{:S(2)}) copy-start(f32[4,64]{1,0:T(4,128)} %get-tuple-element.21) | copy-start | bytes 3076
  472.0 85.3 %copy-start.56 = (f32[4,64]{1,0:T(4,128)S(1)}, f32[4,64]{1,0:T(4,128)}, u32[]{:S(2)}) copy-start(f32[4,64]{1,0:T(4,128)} %get-tuple-element.71) | copy-start | bytes 3076
  472.0 85.5 %copy-start.48 = (f32[1024]{0:T(1024)S(1)}, f32[1024]{0:T(1024)}, u32[]{:S(2)}) copy-start(f32[1024]{0:T(1024)} %get-tuple-element.23) | copy-start | bytes 12292
  472.1 263.9 %all-gather.11.cloned.1.call-start = ((), (), s32[]{:S(2)}) async-start(), calls=%async_computation.17 | async-start | bytes 1572864 | tf_op jit(solution)/shard_map/all_gather | solution.py:236
  472.1 7.4 collective-permute-start.7
  476.3 236.9 %copy-start.7 = (f32[2,128,1024]{2,1,0:T(8,128)S(1)}, f32[2,128,1024]{2,1,0:T(8,128)}, u32[]{:S(2)}) copy-start(f32[2,128,1024]{2,1,0:T(8,128)} %copy-done.6) | copy-start | bytes 3145732
  714.5 24.2 %collective-permute-start.15 = (bf16[128,1024]{1,0:T(8,128)(2,1)S(1)}, bf16[128,1024]{1,0:T(8,128)(2,1)S(1)}, u32[]{:S(2)}, u32[]{:S(2)}) collective-permute-start(bf16[128,1024]{1,0:T(8,128)(2,1)S(1)} %dynamic-slice_bitcast_fusion), channel_id=1, source_target_pairs={{0,4},{4,0},{1,5},{5,1},{2,6},{6,2},{3,7},{7,3},{8,12},{12,8},{9,1... | collective-permute-start | bytes 786440 | tf_op jit(solution)/shard_map/ppermute | solution.py:92
  (29 other events, 178.5 us)
Sparse Core Ops, SparseCore 0:
  13.2 45.7 all-gather.4
  101.6 31.5 reduce-scatter.12
  135.4 80.7 all-gather.6
  217.6 44.7 all-gather.8
  268.4 29.3 reduce-scatter.14
  353.4 30.9 reduce-scatter.16
  388.0 88.2 reduce-scatter.22
  479.9 67.9 reduce-scatter.26
  551.2 61.6 reduce-scatter.24
  616.1 64.5 reduce-scatter.20
  683.2 29.9 reduce-scatter.18
  714.6 21.2 all-gather.10
